TPU v7x, 32 devices: a whole 2x2x4 slice. The times are simulated.
32 devices in a mesh: ep: 8 (over z, x), tp: 4 (over y, core).
Axes of the slice: x: 2, y: 2, z: 4, core: 2. Of those that a mesh axis runs over, the one named last changes fastest.
Arguments:
- tokens: bfloat16 [1024, 3072], P('ep', 'tp'), may hold values from -6 to 6
- expert_ids: int32 [1024, 2], P('ep'), may hold values from 0 to 7, all different within a row
- route_share: float32 [1024], P('ep'), may hold values from 0.5 to 0.95
- w_gate: bfloat16 [65536, 3072], P(('ep', 'tp')), may hold values from -0.109375 to 0.109375
- w_up: bfloat16 [65536, 3072], P(('ep', 'tp')), may hold values from -0.109375 to 0.109375
- w_down: bfloat16 [65536, 3072], P(('ep', 'tp')), may hold values from -0.0625 to 0.0625
- reward_head: float32 [3072], P('tp'), may hold values from -0.109375 to 0.109375
- upstream: bfloat16 [1024, 3072], P('ep', 'tp'), may hold values from -4 to 4
- pair_order: int32 [16], replicated, may hold values from 0 to 15, each once
Outputs:
- layer_out: bfloat16 [1024, 3072], P('ep', 'tp')
- rewards: float32 [16], replicated
- pair_loss: float32 [], replicated
- grad_tokens: bfloat16 [1024, 3072], P('ep', 'tp')
- grad_gate: bfloat16 [65536, 3072], P(('ep', 'tp'))
- grad_up: bfloat16 [65536, 3072], P(('ep', 'tp'))
- grad_down: bfloat16 [65536, 3072], P(('ep', 'tp'))
Inputs may be any that keep to these rules, and one draw needn't show every extreme that they name: `expert_ids`: each row names 2 different experts. `pair_order`: each of the 16 sequence indices appears once.
All inputs are finite; a program needn't handle non-finite values.
Results may differ from a plain program's by a relative error of at most 0.014.
Values may be sent and summed in bfloat16 or wider, within the bound.
A program may use at most 128 MiB of HBM per device.

v0:
```python
import math

import jax
import jax.numpy as jnp
from jax import lax
from jax.sharding import PartitionSpec as P

EXPERTS = 8
SEQ_LEN = 64


loss_scale = 256.0
highest = lax.Precision.HIGHEST


def route_tables(expert_ids, route_share, capacity):
    experts_iota = jnp.arange(EXPERTS, dtype=jnp.int32)
    first_hot = (expert_ids[:, 0:1] == experts_iota[None, :]).astype(jnp.int32)
    second_hot = (expert_ids[:, 1:2] == experts_iota[None, :]).astype(jnp.int32)
    first_rank = jnp.sum((jnp.cumsum(first_hot, axis=0) - first_hot) * first_hot, axis=1)
    second_before = (
        jnp.cumsum(second_hot, axis=0) - second_hot + jnp.sum(first_hot, axis=0)[None, :]
    )
    second_rank = jnp.sum(second_before * second_hot, axis=1)
    route_ranks = jnp.stack([first_rank, second_rank], axis=1)
    route_kept = route_ranks < capacity
    slot_index = jnp.where(route_kept, expert_ids * capacity + route_ranks, -1)
    shares = jnp.stack([route_share, 1.0 - route_share], axis=1) * route_kept.astype(jnp.float32)
    slot_iota = jnp.arange(EXPERTS * capacity, dtype=jnp.int32)
    matches = (slot_index[:, :, None] == slot_iota[None, None, :]).astype(jnp.float32)
    picker = jnp.sum(matches, axis=1)
    mixing = jnp.sum(matches * shares[:, :, None], axis=1)
    return (picker, mixing)


def silu_parts(gate_pre):
    sigmoid_value = jax.nn.sigmoid(gate_pre)
    return (gate_pre * sigmoid_value, sigmoid_value * (1.0 + gate_pre * (1.0 - sigmoid_value)))


def slot_buffer(picker, source_rows, slot_share, replicas, capacity):
    selected = lax.dot_general(
        picker.astype(jnp.bfloat16),
        source_rows,
        (((0,), (0,)), ((), ())),
        preferred_element_type=jnp.float32,
    )
    selected = selected * slot_share[:, None]
    buffer = selected.astype(jnp.bfloat16).reshape(EXPERTS, capacity, source_rows.shape[1])
    return jnp.repeat(buffer, replicas, axis=0)


def gather_slots(picker, source_rows, slot_share, replicas, capacity):
    buffer = slot_buffer(picker, source_rows, slot_share, replicas, capacity)
    arrived = lax.all_to_all(buffer, "ep", split_axis=0, concat_axis=0, tiled=True)
    arrived = lax.all_gather(arrived, "tp", axis=2, tiled=True)
    return arrived.reshape(-1, arrived.shape[2])


def return_sums(term_fn, local_width, replicas, capacity):
    partial_sum = lax.psum_scatter(
        term_fn(jnp.int32(0), lax.axis_size("tp") * local_width).astype(jnp.bfloat16),
        "tp",
        scatter_dimension=0,
        tiled=True,
    ).astype(jnp.float32)
    arrived = lax.all_to_all(
        partial_sum.reshape(local_width, -1, capacity).astype(jnp.bfloat16),
        "ep",
        split_axis=1,
        concat_axis=1,
        tiled=True,
    ).astype(jnp.float32)
    grouped = arrived.reshape(local_width, EXPERTS, replicas, capacity)
    return jnp.sum(grouped, axis=2).reshape(local_width, EXPERTS * capacity)


def per_device(
    tokens, expert_ids, route_share, w_gate, w_up, w_down, reward_head, upstream, pair_order
):
    tok_count, local_width = tokens.shape
    capacity = tok_count * expert_ids.shape[1] // EXPERTS
    replicas = lax.axis_size("ep") // EXPERTS
    picker, mixing = route_tables(expert_ids, route_share, capacity)
    unit_share = jnp.ones((EXPERTS * capacity,), jnp.float32)
    slot_rows = gather_slots(picker, tokens, unit_share, replicas, capacity)
    rows_by_cols = (((1,), (1,)), ((), ()))
    gate_pre = lax.dot_general(slot_rows, w_gate, rows_by_cols, preferred_element_type=jnp.float32)
    up_pre = lax.dot_general(slot_rows, w_up, rows_by_cols, preferred_element_type=jnp.float32)
    silu_value, silu_slope = silu_parts(gate_pre)
    hidden = (silu_value * up_pre).astype(jnp.bfloat16)

    def down_term(first_row, row_count):
        return lax.dot_general(
            w_down, hidden, (((0,), (1,)), ((), ())), preferred_element_type=jnp.float32
        )

    expert_sums = return_sums(down_term, local_width, replicas, capacity)
    mixed_sum = lax.dot_general(
        mixing, expert_sums, rows_by_cols, precision=highest, preferred_element_type=jnp.float32
    )
    layer_out = (tokens.astype(jnp.float32) + mixed_sum).astype(jnp.bfloat16)
    seq_local = tok_count // SEQ_LEN
    seq_total = pair_order.shape[0]
    scores = jnp.dot(layer_out.astype(jnp.float32), reward_head, precision=highest)
    local_rewards = jnp.sum(scores.reshape(seq_local, SEQ_LEN), axis=1) / math.sqrt(SEQ_LEN)
    offset = lax.axis_index("ep") * seq_local
    placed = lax.dynamic_update_slice(
        jnp.zeros((seq_total,), jnp.float32), local_rewards, (offset,)
    )
    rewards = lax.psum(placed, ("ep", "tp"))
    seq_iota = jnp.arange(seq_total, dtype=jnp.int32)
    chosen_hot = (pair_order[0::2][:, None] == seq_iota[None, :]).astype(jnp.float32)
    rejected_hot = (pair_order[1::2][:, None] == seq_iota[None, :]).astype(jnp.float32)
    margin = jnp.dot(chosen_hot, rewards, precision=highest) - jnp.dot(
        rejected_hot, rewards, precision=highest
    )
    pair_loss = jnp.mean(jax.nn.softplus(-margin))
    pair_weight = jax.nn.sigmoid(-margin)
    seq_coef = jnp.dot(pair_weight, rejected_hot - chosen_hot, precision=highest)
    token_coef = jnp.repeat(lax.dynamic_slice_in_dim(seq_coef, offset, seq_local), SEQ_LEN)
    grad_out = (
        upstream.astype(jnp.float32)
        + loss_scale * token_coef[:, None] * reward_head[None, :] / math.sqrt(SEQ_LEN)
    ).astype(jnp.bfloat16)
    slot_share = jnp.sum(mixing, axis=0)
    grad_slots = gather_slots(picker, grad_out, slot_share, replicas, capacity)
    hidden_grad = lax.dot_general(
        grad_slots, w_down, rows_by_cols, preferred_element_type=jnp.float32
    )
    gate_grad = (hidden_grad * up_pre * silu_slope).astype(jnp.bfloat16)
    up_grad = (hidden_grad * silu_value).astype(jnp.bfloat16)
    over_slots = (((0,), (0,)), ((), ()))
    grad_down = lax.dot_general(
        hidden, grad_slots, over_slots, preferred_element_type=jnp.float32
    ).astype(jnp.bfloat16)
    grad_gate = lax.dot_general(
        gate_grad, slot_rows, over_slots, preferred_element_type=jnp.float32
    ).astype(jnp.bfloat16)
    grad_up = lax.dot_general(
        up_grad, slot_rows, over_slots, preferred_element_type=jnp.float32
    ).astype(jnp.bfloat16)

    def input_term(first_row, row_count):
        across = (((0,), (1,)), ((), ()))
        return lax.dot_general(
            w_gate, gate_grad, across, preferred_element_type=jnp.float32
        ) + lax.dot_general(w_up, up_grad, across, preferred_element_type=jnp.float32)

    input_sums = return_sums(input_term, local_width, replicas, capacity)
    returned = lax.dot_general(
        picker, input_sums, rows_by_cols, precision=highest, preferred_element_type=jnp.float32
    )
    grad_tokens = (grad_out.astype(jnp.float32) + returned).astype(jnp.bfloat16)
    return (layer_out, rewards, pair_loss, grad_tokens, grad_gate, grad_up, grad_down)


def solution(mesh):
    in_specs = (
        P("ep", "tp"),
        P("ep", None),
        P("ep"),
        P(("ep", "tp"), None),
        P(("ep", "tp"), None),
        P(("ep", "tp"), None),
        P("tp"),
        P("ep", "tp"),
        P(),
    )
    out_specs = (
        P("ep", "tp"),
        P(),
        P(),
        P("ep", "tp"),
        P(("ep", "tp"), None),
        P(("ep", "tp"), None),
        P(("ep", "tp"), None),
    )
    return jax.shard_map(
        per_device, mesh=mesh, in_specs=in_specs, out_specs=out_specs, check_vma=False
    )
```

profile of v0, /device:TPU:0, one launch (start us, length us, event | category | flops | bytes accessed | tf_op | source)
XLA Modules:
  0.0 279.3 jit_solution(15317795496625174167)
XLA Ops:
  7.2 0.7 subtract_bitcast_fusion
  7.9 0.8 slice_bitcast_fusion.1
  9.4 0.7 add_select_fusion
  10.1 0.7 maximum_select_fusion
  11.0 1.2 convolution_convert_fusion.4
  12.2 19.2 %all_to_all.20 = bf16[8,32,768]{2,1,0:T(8,128)(2,1)} all-to-all(bf16[8,32,768]{2,1,0:T(8,128)(2,1)S(1)} %bitcast.75), channel_id=1, replica_groups=mesh['ep'=8,'tp'=4] {'ep'}, dimensions={0} | all-to-all | bytes 786432 | tf_op jit(solution)/shard_map/all_to_all | solution.py:55
  31.5 18.4 %all-gather.3.cloned.1.call-done = bf16[8,32,3072]{2,1,0:T(8,128)(2,1)} async-done(((bf16[8,32,768]{2,1,0:T(8,128)(2,1)}), bf16[8,32,3072]{2,1,0:T(8,128)(2,1)}) %all-gather.3.cloned.1.call-update) | async-done | bytes 1572880 | tf_op jit(solution)/shard_map/all_gather | solution.py:56
  49.9 8.5 %fusion.30 = f32[256,2048]{1,0:T(8,128)S(1)} fusion(bf16[256,3072]{1,0:T(8,128)(2,1)} %bitcast.67, bf16[2048,3072]{1,0:T(8,128)(2,1)} %param.12), kind=kOutput, calls=%fused_computation.68 | convolution fusion | flops 3221225472 | bytes 16252928 | tf_op jit(solution)/shard_map/dot_general | solution.py:88
  58.5 10.3 %multiply_convert_fusion.2 = (bf16[256,2048]{1,0:T(8,128)(2,1)S(1)}, f32[256,2048]{1,0:T(8,128)}) fusion(f32[256,2048]{1,0:T(8,128)S(1)} %fusion.30, bf16[256,3072]{1,0:T(8,128)(2,1)S(1)} %bitcast.68, bf16[2048,3072]{1,0:T(8,128)(2,1)} %param.13), kind=kOutput, calls=%fused_computation.10 | convolution fusion | flops 3224371200 | bytes 19398656 | tf_op jit(solution)/shard_map/dot_general | solution.py:89
  68.8 1.0 copy-done.2
  69.7 9.1 %fusion.1 = bf16[3072,256]{0,1:T(8,128)(2,1)} fusion(bf16[256,2048]{1,0:T(8,128)(2,1)S(1)} %get-tuple-element.16, bf16[2048,3072]{1,0:T(8,128)(2,1)} %param.14), kind=kOutput, calls=%fused_computation.6 | convolution fusion | flops 3222011904 | bytes 15204352 | tf_op jit(solution)/shard_map/dot_general | solution.py:94
  78.8 28.1 %reduce-scatter.3.cloned.1.call-done = bf16[768,256]{0,1:T(8,128)(2,1)} async-done(((bf16[3072,256]{0,1:T(8,128)(2,1)}), bf16[768,256]{0,1:T(8,128)(2,1)}) %reduce-scatter.3.cloned.1.call-update) | async-done | bytes 393232 | tf_op jit(solution)/shard_map/reduce_scatter | solution.py:61
  107.0 5.5 %all-to-all-start.1 = ((bf16[768,8,32]{0,2,1:T(8,128)(2,1)}), bf16[768,8,32]{0,2,1:T(8,128)(2,1)S(1)}, u32[]{:S(2)}, u32[]{:S(2)}) async-start(bf16[768,8,32]{0,2,1:T(8,128)(2,1)} %bitcast.76), calls=%async_computation.2 | async-start | bytes 786432 | tf_op jit(solution)/shard_map/all_to_all | solution.py:67
  112.6 11.4 %all-to-all-done.1 = bf16[768,8,32]{0,2,1:T(8,128)(2,1)S(1)} async-done(((bf16[768,8,32]{0,2,1:T(8,128)(2,1)}), bf16[768,8,32]{0,2,1:T(8,128)(2,1)S(1)}, u32[]{:S(2)}, u32[]{:S(2)}) %all-to-all-start.1) | async-done | bytes 393248 | tf_op jit(solution)/shard_map/all_to_all | solution.py:67
  124.1 0.3 fusion.5
  125.1 38.5 %psum.7 = f32[16]{0:T(128)S(1)} all-reduce(f32[16]{0:T(128)S(1)} %multiply_dynamic-update-slice_fusion), channel_id=1, replica_groups=mesh['ep'=8,'tp'=4] {'ep','tp'}, use_global_device_ids=true, to_apply=%region_9.10 | all-reduce | flops 16 | bytes 128 | tf_op jit(solution)/shard_map/psum | solution.py:111
  163.8 0.8 fusion.20
  165.1 0.3 fusion.4
  165.4 15.3 %all_to_all.21 = bf16[8,32,768]{2,1,0:T(8,128)(2,1)} all-to-all(bf16[8,32,768]{2,1,0:T(8,128)(2,1)S(1)} %bitcast.78), channel_id=1, replica_groups=mesh['ep'=8,'tp'=4] {'ep'}, dimensions={0} | all-to-all | bytes 786432 | tf_op jit(solution)/shard_map/all_to_all | solution.py:55
  180.8 0.2 reduce-scatter.5.cloned.1.call-start
  181.0 17.7 %all-gather.5.cloned.1.call-done = bf16[8,32,3072]{2,1,0:T(8,128)(2,1)} async-done(((bf16[8,32,768]{2,1,0:T(8,128)(2,1)}), bf16[8,32,3072]{2,1,0:T(8,128)(2,1)}) %all-gather.5.cloned.1.call-update) | async-done | bytes 1572880 | tf_op jit(solution)/shard_map/all_gather | solution.py:56
  198.7 10.2 %multiply_convert_fusion = (bf16[256,2048]{1,0:T(8,128)(2,1)S(1)}, bf16[256,2048]{1,0:T(8,128)(2,1)S(1)}) fusion(f32[256,2048]{1,0:T(8,128)} %copy-done.13, f32[256,2048]{1,0:T(8,128)} %get-tuple-element.17, bf16[256,3072]{1,0:T(8,128)(2,1)} %bitcast.71, bf16[2048,3072]{1,0:T(8,128)(2,1)} %param.14), kind=kOutput, calls=%fused_computation.8 | convolution fusion | flops 3228041216 | bytes 20447232 | tf_op jit(solution)/shard_map/dot_general | solution.py:128
  208.9 7.2 %fusion.31 = f32[256,3072]{1,0:T(8,128)S(1)} fusion(bf16[256,2048]{1,0:T(8,128)(2,1)S(1)} %get-tuple-element.13, bf16[2048,3072]{1,0:T(8,128)(2,1)} %param.12), kind=kOutput, calls=%fused_computation.69 | convolution fusion | flops 3221225472 | bytes 16777216 | tf_op jit(solution)/shard_map/dot_general | solution.py:146
  216.1 9.3 %fusion.2 = bf16[3072,256]{0,1:T(8,128)(2,1)} fusion(f32[256,3072]{1,0:T(8,128)S(1)} %fusion.31, bf16[256,2048]{1,0:T(8,128)(2,1)S(1)} %get-tuple-element.12, bf16[2048,3072]{1,0:T(8,128)(2,1)} %param.13), kind=kOutput, calls=%fused_computation.7 | convolution fusion | flops 3222798336 | bytes 18350080 | tf_op jit(solution)/shard_map/dot_general | solution.py:148
  226.2 0.6 copy-done.1
  226.8 7.9 %convolution_convert_fusion = bf16[2048,3072]{1,0:T(8,128)(2,1)} fusion(bf16[256,2048]{1,0:T(8,128)(2,1)} %copy-done.2, bf16[256,3072]{1,0:T(8,128)(2,1)S(1)} %bitcast.72), kind=kOutput, calls=%fused_computation | convolution fusion | flops 3227516928 | bytes 15204352 | tf_op jit(solution)/shard_map/dot_general | solution.py:134
  234.8 6.6 %convolution_convert_fusion.1 = bf16[2048,3072]{1,0:T(8,128)(2,1)} fusion(bf16[256,2048]{1,0:T(8,128)(2,1)S(1)} %copy-done.6, bf16[256,3072]{1,0:T(8,128)(2,1)S(1)} %bitcast.69), kind=kOutput, calls=%fused_computation.1 | convolution fusion | flops 3227516928 | bytes 15204352 | tf_op jit(solution)/shard_map/dot_general | solution.py:140
  241.4 12.2 %reduce-scatter.5.cloned.1.call-done = bf16[768,256]{0,1:T(8,128)(2,1)} async-done(((bf16[3072,256]{0,1:T(8,128)(2,1)}), bf16[768,256]{0,1:T(8,128)(2,1)}) %reduce-scatter.5.cloned.1.call-update) | async-done | bytes 393232 | tf_op jit(solution)/shard_map/reduce_scatter | solution.py:61
  253.6 5.5 %all-to-all-start.3 = ((bf16[768,8,32]{0,2,1:T(8,128)(2,1)}), bf16[768,8,32]{0,2,1:T(8,128)(2,1)S(1)}, u32[]{:S(2)}, u32[]{:S(2)}) async-start(bf16[768,8,32]{0,2,1:T(8,128)(2,1)} %bitcast.77), calls=%async_computation.5 | async-start | bytes 786432 | tf_op jit(solution)/shard_map/all_to_all | solution.py:67
  259.1 6.6 %convolution_convert_fusion.2 = bf16[2048,3072]{1,0:T(8,128)(2,1)} fusion(bf16[256,2048]{1,0:T(8,128)(2,1)S(1)} %copy-done.4, bf16[256,3072]{1,0:T(8,128)(2,1)S(1)} %bitcast.70), kind=kOutput, calls=%fused_computation.2 | convolution fusion | flops 3227516928 | bytes 15204352 | tf_op jit(solution)/shard_map/dot_general | solution.py:137
  265.7 4.9 %all-to-all-done.3 = bf16[768,8,32]{0,2,1:T(8,128)(2,1)S(1)} async-done(((bf16[768,8,32]{0,2,1:T(8,128)(2,1)}), bf16[768,8,32]{0,2,1:T(8,128)(2,1)S(1)}, u32[]{:S(2)}, u32[]{:S(2)}) %all-to-all-start.3) | async-done | bytes 393248 | tf_op jit(solution)/shard_map/all_to_all | solution.py:67
  270.6 1.0 fusion.6
  (52 shorter events, 2.6 us)
Async XLA Ops:
  7.2 42.8 %all-gather.3.cloned.1.call-start = ((), (), s32[]{:S(2)}) async-start(), calls=%async_computation.6 | async-start | bytes 1966080 | tf_op jit(solution)/shard_map/all_gather | solution.py:56
  31.4 75.6 %reduce-scatter.3.cloned.1.call-start = ((), (), s32[]{:S(2)}) async-start(), calls=%async_computation.7 | async-start | bytes 1966080 | tf_op jit(solution)/shard_map/reduce_scatter | solution.py:61
  49.9 8.6 %copy-start = (bf16[8,32,3072]{2,1,0:T(8,128)(2,1)S(1)}, bf16[8,32,3072]{2,1,0:T(8,128)(2,1)}, u32[]{:S(2)}) copy-start(bf16[8,32,3072]{2,1,0:T(8,128)(2,1)} %all-gather.3.cloned.1.call-done) | copy-start | bytes 4718596
  58.5 10.3 %copy-start.13 = (f32[256,2048]{1,0:T(8,128)}, f32[256,2048]{1,0:T(8,128)S(1)}, u32[]{:S(2)}) copy-start(f32[256,2048]{1,0:T(8,128)S(1)} %fusion.30) | copy-start | bytes 6291460
  68.8 1.0 copy-start.2
  78.8 33.7 %copy-start.11 = (s32[16]{0:T(128)S(1)}, s32[16]{0:T(128)}, u32[]{:S(2)}) copy-start(s32[16]{0:T(128)} %param.17) | copy-start | bytes 196
  78.8 33.8 %copy-start.10 = (f32[768]{0:T(1024)S(1)}, f32[768]{0:T(1024)}, u32[]{:S(2)}) copy-start(f32[768]{0:T(1024)} %param.15) | copy-start | bytes 9220
  78.8 45.2 %copy-start.8 = (bf16[128,768]{1,0:T(8,128)(2,1)S(1)}, bf16[128,768]{1,0:T(8,128)(2,1)}, u32[]{:S(2)}) copy-start(bf16[128,768]{1,0:T(8,128)(2,1)} %param.9) | copy-start | bytes 589828
  78.8 86.3 %copy-start.9 = (bf16[128,768]{1,0:T(8,128)(2,1)S(1)}, bf16[128,768]{1,0:T(8,128)(2,1)}, u32[]{:S(2)}) copy-start(bf16[128,768]{1,0:T(8,128)(2,1)} %param.16) | copy-start | bytes 589828
  107.0 17.1 %all-to-all-start.1 = ((bf16[768,8,32]{0,2,1:T(8,128)(2,1)}), bf16[768,8,32]{0,2,1:T(8,128)(2,1)S(1)}, u32[]{:S(2)}, u32[]{:S(2)}) async-start(bf16[768,8,32]{0,2,1:T(8,128)(2,1)} %bitcast.76), calls=%async_computation.2 | async-start | bytes 786432 | tf_op jit(solution)/shard_map/all_to_all | solution.py:67
  112.5 86.2 %all-gather.5.cloned.1.call-start = ((), (), s32[]{:S(2)}) async-start(), calls=%async_computation.8 | async-start | bytes 1966080 | tf_op jit(solution)/shard_map/all_gather | solution.py:56
  124.4 84.5 %copy-start.7 = (bf16[128,768]{1,0:T(8,128)(2,1)}, bf16[128,768]{1,0:T(8,128)(2,1)S(1)}, u32[]{:S(2)}) copy-start(bf16[128,768]{1,0:T(8,128)(2,1)S(1)} %fusion.5) | copy-start | bytes 589828
  163.6 45.2 %copy-start.12 = (f32[16]{0:T(128)}, f32[16]{0:T(128)S(1)}, u32[]{:S(2)}) copy-start(f32[16]{0:T(128)S(1)} %psum.7) | copy-start | bytes 196
  180.8 72.8 %reduce-scatter.5.cloned.1.call-start = ((), (), s32[]{:S(2)}) async-start(), calls=%async_computation.9 | async-start | bytes 1966080 | tf_op jit(solution)/shard_map/reduce_scatter | solution.py:61
  208.9 7.2 %copy-start.3 = (bf16[256,2048]{1,0:T(8,128)(2,1)}, bf16[256,2048]{1,0:T(8,128)(2,1)S(1)}, u32[]{:S(2)}) copy-start(bf16[256,2048]{1,0:T(8,128)(2,1)S(1)} %get-tuple-element.13) | copy-start | bytes 3145732
  208.9 7.2 %copy-start.5 = (bf16[256,2048]{1,0:T(8,128)(2,1)}, bf16[256,2048]{1,0:T(8,128)(2,1)S(1)}, u32[]{:S(2)}) copy-start(bf16[256,2048]{1,0:T(8,128)(2,1)S(1)} %get-tuple-element.12) | copy-start | bytes 3145732
  225.4 1.4 copy-start.1
  226.8 7.9 %copy-start.6 = (bf16[256,2048]{1,0:T(8,128)(2,1)S(1)}, bf16[256,2048]{1,0:T(8,128)(2,1)}, u32[]{:S(2)}) copy-start(bf16[256,2048]{1,0:T(8,128)(2,1)} %copy-done.5) | copy-start | bytes 3145732
  234.8 24.3 %copy-start.4 = (bf16[256,2048]{1,0:T(8,128)(2,1)S(1)}, bf16[256,2048]{1,0:T(8,128)(2,1)}, u32[]{:S(2)}) copy-start(bf16[256,2048]{1,0:T(8,128)(2,1)} %copy-done.3) | copy-start | bytes 3145732
  253.6 17.0 %all-to-all-start.3 = ((bf16[768,8,32]{0,2,1:T(8,128)(2,1)}), bf16[768,8,32]{0,2,1:T(8,128)(2,1)S(1)}, u32[]{:S(2)}, u32[]{:S(2)}) async-start(bf16[768,8,32]{0,2,1:T(8,128)(2,1)} %bitcast.77), calls=%async_computation.5 | async-start | bytes 786432 | tf_op jit(solution)/shard_map/all_to_all | solution.py:67
Sparse Core Ops, SparseCore 0:
  31.6 18.3 all-gather.2
  79.0 27.9 reduce-scatter.2
  180.9 17.7 all-gather.4
  225.6 27.9 reduce-scatter.4
where the time goes:
time: 280 us; the launch traced here: 279 us
  waiting for transfers between devices  92.9 us (33%)
  matrix products  80 us (29%)
  blocking collectives  73.1 us (26%)
  between operations  15.9 us (6%)
  starting transfers between devices  11.3 us (4%)
  other arithmetic  3.33 us (1%)
  local copies, waits for them, and re-layouts  2.84 us (1%)
    reduce_scatter x2, waiting for transfers between devices, return_sums(): lax.psum_scatter(term_fn(jnp.int32(0), lax.axis_size('tp') * local_width)...  40.3 us
    psum x1, blocking collectives, per_device(): rewards = lax.psum(placed, ('ep', 'tp'))  38.5 us
    all_gather x2, waiting for transfers between devices, gather_slots(): arrived = lax.all_gather(arrived, 'tp', axis=2, tiled=True)  36.1 us
    all_to_all x2, blocking collectives, gather_slots(): lax.all_to_all(buffer, 'ep', split_axis=0, concat_axis=0, tiled=True)  34.5 us
    all_to_all x2, waiting for transfers between devices, return_sums(): lax.all_to_all(partial_sum.reshape(local_width, -1, capacity).astype(jnp....  16.3 us
    all_to_all x2, starting transfers between devices, return_sums(): lax.all_to_all(partial_sum.reshape(local_width, -1, capacity).astype(jnp....  11 us
    dot_general x1, matrix products, per_device(): lax.dot_general(slot_rows, w_up, rows_by_cols, preferred_element_type=jnp...  10.3 us
    dot_general x1, matrix products, per_device(): lax.dot_general(grad_slots, w_down, rows_by_cols, preferred_element_type=...  10.2 us
  transfers between devices with their start and end apart: 6, of which 6 were waited for; matrix products, arithmetic and copies ran while one was open for 8% of the time, Pallas kernels for 0%

commit v1 on v0

v1 whole, which is shorter than its diff:
```python
import math
from functools import partial

import jax
import jax.numpy as jnp
from jax import lax
from jax.experimental import pallas as pl
from jax.experimental.pallas import tpu as pltpu
from jax.sharding import PartitionSpec as P

EXPERTS = 8
SEQ_LEN = 64


loss_scale = 256.0
highest = lax.Precision.HIGHEST


def route_tables(expert_ids, route_share, capacity):
    experts_iota = jnp.arange(EXPERTS, dtype=jnp.int32)
    first_hot = (expert_ids[:, 0:1] == experts_iota[None, :]).astype(jnp.int32)
    second_hot = (expert_ids[:, 1:2] == experts_iota[None, :]).astype(jnp.int32)
    first_rank = jnp.sum((jnp.cumsum(first_hot, axis=0) - first_hot) * first_hot, axis=1)
    second_before = (
        jnp.cumsum(second_hot, axis=0) - second_hot + jnp.sum(first_hot, axis=0)[None, :]
    )
    second_rank = jnp.sum(second_before * second_hot, axis=1)
    route_ranks = jnp.stack([first_rank, second_rank], axis=1)
    route_kept = route_ranks < capacity
    slot_index = jnp.where(route_kept, expert_ids * capacity + route_ranks, -1)
    shares = jnp.stack([route_share, 1.0 - route_share], axis=1) * route_kept.astype(jnp.float32)
    slot_iota = jnp.arange(EXPERTS * capacity, dtype=jnp.int32)
    matches = (slot_index[:, :, None] == slot_iota[None, None, :]).astype(jnp.float32)
    picker = jnp.sum(matches, axis=1)
    mixing = jnp.sum(matches * shares[:, :, None], axis=1)
    return (picker, mixing)


def silu_parts(gate_pre):
    sigmoid_value = jax.nn.sigmoid(gate_pre)
    return (gate_pre * sigmoid_value, sigmoid_value * (1.0 + gate_pre * (1.0 - sigmoid_value)))


def slot_buffer(picker, source_rows, capacity):
    selected = lax.dot_general(
        picker.astype(jnp.bfloat16),
        source_rows,
        (((0,), (0,)), ((), ())),
        preferred_element_type=jnp.float32,
    )
    return selected.astype(jnp.bfloat16).reshape(EXPERTS, capacity, source_rows.shape[1])


MESH = pl.DeviceIdType.MESH


def remote(src, dst, send_sem, recv_sem, target):
    return pltpu.make_async_remote_copy(
        src_ref=src,
        dst_ref=dst,
        send_sem=send_sem,
        recv_sem=recv_sem,
        device_id=target,
        device_id_type=MESH,
    )


def spread_kernel(
    n_ep, n_tp, tok_ref, ups_ref, meta_ref, head_ref, tok_out, ups_out, meta_out, head_out,
    local_sem, tok_send, ups_send, meta_send, head_send, tp_send,
    tok_recv, ups_recv, meta_recv, head_recv, tp_recv,
):
    q = lax.axis_index("ep")
    t = lax.axis_index("tp")
    width = tok_ref.shape[2]
    replicas = n_ep // tok_ref.shape[0]
    partner = t + 1 - 2 * (t % 2)

    barrier = pltpu.get_barrier_semaphore()
    for k in range(1, n_ep):
        pl.semaphore_signal(barrier, inc=1, device_id=((q + k) % n_ep, t), device_id_type=MESH)
    for k in range(1, n_tp):
        pl.semaphore_signal(barrier, inc=1, device_id=(q, (t + k) % n_tp), device_id_type=MESH)
    pl.semaphore_wait(barrier, n_ep + n_tp - 2)

    def columns(owner):
        return pl.ds(pl.multiple_of(owner * width, 128), width)

    own = q // replicas
    local = [
        pltpu.make_async_copy(tok_ref.at[own], tok_out.at[q, :, columns(t)], local_sem.at[0]),
        pltpu.make_async_copy(ups_ref.at[own], ups_out.at[q], local_sem.at[1]),
        pltpu.make_async_copy(meta_ref.at[own], meta_out.at[q], local_sem.at[2]),
        pltpu.make_async_copy(head_ref, head_out.at[t], local_sem.at[3]),
    ]
    for copy in local:
        copy.start()
    for k in range(1, n_ep):
        to = (q + k) % n_ep
        remote(
            tok_ref.at[to // replicas], tok_out.at[q, :, columns(t)],
            tok_send, tok_recv.at[k], (to, t),
        ).start()
    for k in range(1, n_tp):
        remote(
            head_ref, head_out.at[t], head_send, head_recv.at[k], (q, (t + k) % n_tp)
        ).start()
    for k in range(1, n_ep):
        to = (q + k) % n_ep
        remote(
            meta_ref.at[to // replicas], meta_out.at[q], meta_send, meta_recv.at[k], (to, t)
        ).start()
        remote(
            ups_ref.at[to // replicas], ups_out.at[q], ups_send, ups_recv.at[k], (to, t)
        ).start()

    def hand_on(k, owner, target, row):
        piece = tok_out.at[(q + n_ep - k) % n_ep, :, columns(owner)]
        return remote(piece, piece, tp_send, tp_recv.at[row, k], (q, target))

    def forward(k):
        for j in range(1, n_tp // 2):
            origin = (t + n_tp - 2 * j) % n_tp
            hand_on(k, origin, t, j - 1).wait_recv()
            hand_on(k, origin, partner, n_tp // 2 - 1 + j).start()

    lag = 2
    for k in range(n_ep):
        if k == 0:
            local[0].wait()
        else:
            source = (q + n_ep - k) % n_ep
            remote(
                tok_ref.at[0], tok_out.at[source, :, columns(t)],
                tok_send, tok_recv.at[k], (source, t),
            ).wait_recv()
        for j in range(1, n_tp // 2):
            hand_on(k, t, (t + 2 * j) % n_tp, j - 1).start()
        hand_on(k, t, partner, n_tp // 2 - 1).start()
        if k >= lag:
            forward(k - lag)
    for k in range(max(n_ep - lag, 0), n_ep):
        forward(k)
    for k in range(n_ep):
        hand_on(k, partner, t, n_tp // 2 - 1).wait_recv()
        for j in range(1, n_tp // 2):
            origin = (partner + n_tp - 2 * j) % n_tp
            hand_on(k, origin, t, n_tp // 2 - 1 + j).wait_recv()
    for copy in local[1:]:
        copy.wait()
    for k in range(1, n_tp):
        source = (t + n_tp - k) % n_tp
        remote(head_ref, head_out.at[source], head_send, head_recv.at[k], (q, source)).wait_recv()
    for k in range(1, n_ep):
        source = (q + n_ep - k) % n_ep
        remote(
            meta_ref.at[0], meta_out.at[source], meta_send, meta_recv.at[k], (source, t)
        ).wait_recv()
        remote(
            ups_ref.at[0], ups_out.at[source], ups_send, ups_recv.at[k], (source, t)
        ).wait_recv()

    def drain(sent, sem):
        pltpu.make_async_copy(sent, sent, sem).wait()

    drain(ups_out.at[pl.ds(0, n_ep - 1)], tok_send)
    drain(ups_out.at[pl.ds(0, n_ep - 1)], ups_send)
    drain(meta_out.at[pl.ds(0, n_ep - 1)], meta_send)
    drain(head_out.at[pl.ds(0, n_tp - 1)], head_send)
    drain(tok_out.at[:, :, pl.ds(0, (n_tp - 1) * width)], tp_send)


def spread_slots(tok_buf, ups_buf, meta, head_rows):
    n_ep = lax.axis_size("ep")
    n_tp = lax.axis_size("tp")
    experts, capacity, width = tok_buf.shape
    dma = pltpu.SemaphoreType.DMA
    vmem = pl.BlockSpec(memory_space=pltpu.VMEM)
    return pl.pallas_call(
        partial(spread_kernel, n_ep, n_tp),
        out_shape=(
            jax.ShapeDtypeStruct((n_ep, capacity, n_tp * width), jnp.bfloat16),
            jax.ShapeDtypeStruct((n_ep, capacity, width), jnp.bfloat16),
            jax.ShapeDtypeStruct((n_ep,) + meta.shape[1:], jnp.float32),
            jax.ShapeDtypeStruct((n_tp,) + head_rows.shape, jnp.float32),
        ),
        in_specs=[vmem] * 4,
        out_specs=[vmem] * 4,
        scratch_shapes=[
            dma((4,)), dma, dma, dma, dma, dma,
            dma((n_ep,)), dma((n_ep,)), dma((n_ep,)), dma((n_tp,)), dma((n_tp - 1, n_ep)),
        ],
        compiler_params=pltpu.CompilerParams(collective_id=0, has_side_effects=True),
        name="spread_slots",
    )(tok_buf, ups_buf, meta, head_rows)


def share_kernel(n_ep, n_tp, mine_ref, all_ref, local_sem, send_sem, recv_sem):
    q = lax.axis_index("ep")
    t = lax.axis_index("tp")
    count = n_ep * n_tp
    me = q * n_tp + t
    barrier = pltpu.get_barrier_semaphore()

    def greet(k, carry):
        other = (me + k) % count
        pl.semaphore_signal(
            barrier, inc=1, device_id=(other // n_tp, other % n_tp), device_id_type=MESH
        )
        return carry

    lax.fori_loop(1, count, greet, 0)
    pl.semaphore_wait(barrier, count - 1)
    own = pltpu.make_async_copy(mine_ref, all_ref.at[me], local_sem)
    own.start()

    def send(k, carry):
        other = (me + k) % count
        remote(
            mine_ref, all_ref.at[me], send_sem, recv_sem, (other // n_tp, other % n_tp)
        ).start()
        return carry

    lax.fori_loop(1, count, send, 0)
    own.wait()
    rest = all_ref.at[pl.ds(0, count - 1)]
    pltpu.make_async_copy(rest, rest, recv_sem).wait()
    pltpu.make_async_copy(rest, rest, send_sem).wait()


def share_rows(mine):
    n_ep = lax.axis_size("ep")
    n_tp = lax.axis_size("tp")
    dma = pltpu.SemaphoreType.DMA
    vmem = pl.BlockSpec(memory_space=pltpu.VMEM)
    return pl.pallas_call(
        partial(share_kernel, n_ep, n_tp),
        out_shape=jax.ShapeDtypeStruct((n_ep * n_tp,) + mine.shape, jnp.float32),
        in_specs=[vmem],
        out_specs=vmem,
        scratch_shapes=[dma, dma, dma],
        compiler_params=pltpu.CompilerParams(collective_id=1, has_side_effects=True),
        name="share_rows",
    )(mine)


def return_sums(sums, local_width, replicas, capacity):
    partial_sum = lax.psum_scatter(
        sums,
        "tp",
        scatter_dimension=0,
        tiled=True,
    ).astype(jnp.float32)
    arrived = lax.all_to_all(
        partial_sum.reshape(local_width, -1, capacity).astype(jnp.bfloat16),
        "ep",
        split_axis=1,
        concat_axis=1,
        tiled=True,
    ).astype(jnp.float32)
    grouped = arrived.reshape(local_width, EXPERTS, replicas, capacity)
    return jnp.sum(grouped, axis=2).reshape(local_width, EXPERTS * capacity)


def per_device(
    tokens, expert_ids, route_share, w_gate, w_up, w_down, reward_head, upstream, pair_order
):
    tok_count, local_width = tokens.shape
    capacity = tok_count * expert_ids.shape[1] // EXPERTS
    n_ep = lax.axis_size("ep")
    replicas = n_ep // EXPERTS
    seq_local = tok_count // SEQ_LEN
    seq_total = pair_order.shape[0]
    seq_scale = loss_scale / math.sqrt(SEQ_LEN)
    picker, mixing = route_tables(expert_ids, route_share, capacity)
    tok_buf = slot_buffer(picker, tokens, capacity)
    ups_buf = slot_buffer(picker, upstream, capacity)
    seq_share = jnp.sum(mixing.reshape(seq_local, SEQ_LEN, EXPERTS, capacity), axis=1)
    meta = jnp.zeros((EXPERTS, 8 * pl.cdiv(seq_local, 8), 128 * pl.cdiv(capacity, 128)), jnp.float32)
    meta = meta.at[:, :seq_local, :capacity].set(seq_share.transpose(1, 0, 2))
    slot_rows, ups_part, meta_all, head_all = spread_slots(
        tok_buf, ups_buf, meta, reward_head.reshape(-1, 128)
    )
    width = slot_rows.shape[2]
    slot_rows = slot_rows.reshape(-1, width)
    ups_rows = lax.all_gather(ups_part, "tp", axis=2, tiled=True).reshape(-1, width)
    head_full = head_all.reshape(width)
    slot_meta = meta_all[:, :seq_local, :capacity]

    rows_by_cols = (((1,), (1,)), ((), ()))
    gate_pre = lax.dot_general(slot_rows, w_gate, rows_by_cols, preferred_element_type=jnp.float32)
    up_pre = lax.dot_general(slot_rows, w_up, rows_by_cols, preferred_element_type=jnp.float32)
    silu_value, silu_slope = silu_parts(gate_pre)
    hidden = (silu_value * up_pre).astype(jnp.bfloat16)

    def down_term(first_row, row_count):
        return lax.dot_general(
            w_down, hidden, (((0,), (1,)), ((), ())), preferred_element_type=jnp.float32
        )

    down_sums = down_term(0, 0).astype(jnp.bfloat16)
    down_sums, ups_rows, head_full = lax.optimization_barrier((down_sums, ups_rows, head_full))
    expert_sums = return_sums(down_sums, local_width, replicas, capacity)

    ups_cols = lax.dot_general(ups_rows, w_down, rows_by_cols, preferred_element_type=jnp.float32)
    head_parts = []
    head_rest = head_full
    for _ in range(3):
        part = lax.reduce_precision(head_rest, 8, 7)
        head_parts.append(part.astype(jnp.bfloat16))
        head_rest = head_rest - part
    head_cols = jnp.sum(
        lax.dot_general(
            jnp.stack(head_parts), w_down, rows_by_cols, preferred_element_type=jnp.float32
        ),
        axis=0,
    )

    slot_scores = jnp.sum(hidden.astype(jnp.float32) * head_cols[None, :], axis=1)
    expert_part = jnp.sum(slot_meta * slot_scores.reshape(n_ep, 1, capacity), axis=2).reshape(-1)
    own_scores = jnp.sum(tokens.astype(jnp.float32) * reward_head[None, :], axis=1)
    own_part = jnp.sum(own_scores.reshape(seq_local, SEQ_LEN), axis=1)
    offset = lax.axis_index("ep") * seq_local
    placed = lax.dynamic_update_slice(jnp.zeros((seq_total,), jnp.float32), own_part, (offset,))
    lanes = 1024 * pl.cdiv(seq_total, 1024)
    mine = jnp.pad(placed + expert_part, (0, lanes - seq_total)).reshape(-1, 128)
    gathered = share_rows(mine)
    rewards = jnp.sum(gathered, axis=0).reshape(-1)[:seq_total] / math.sqrt(SEQ_LEN)

    seq_iota = jnp.arange(seq_total, dtype=jnp.int32)
    chosen_hot = (pair_order[0::2][:, None] == seq_iota[None, :]).astype(jnp.float32)
    rejected_hot = (pair_order[1::2][:, None] == seq_iota[None, :]).astype(jnp.float32)
    margin = jnp.sum((chosen_hot - rejected_hot) * rewards[None, :], axis=1)
    pair_loss = jnp.mean(jax.nn.softplus(-margin))
    pair_weight = jax.nn.sigmoid(-margin)
    seq_coef = jnp.sum(pair_weight[:, None] * (rejected_hot - chosen_hot), axis=0)
    token_coef = jnp.repeat(lax.dynamic_slice_in_dim(seq_coef, offset, seq_local), SEQ_LEN)
    grad_out = (
        upstream.astype(jnp.float32) + seq_scale * token_coef[:, None] * reward_head[None, :]
    ).astype(jnp.bfloat16)

    slot_share = jnp.sum(slot_meta, axis=1).reshape(-1, 1)
    coef_of = seq_coef.reshape(n_ep, seq_local, 1)
    slot_coef = seq_scale * jnp.sum(jnp.where(slot_meta > 0.0, coef_of, 0.0), axis=1).reshape(-1, 1)
    slot_out = (ups_rows.astype(jnp.float32) + slot_coef * head_full[None, :]).astype(jnp.bfloat16)
    grad_slots = (slot_share * slot_out.astype(jnp.float32)).astype(jnp.bfloat16)
    hidden_grad = slot_share * (ups_cols + slot_coef * head_cols[None, :])
    gate_grad = (hidden_grad * up_pre * silu_slope).astype(jnp.bfloat16)
    up_grad = (hidden_grad * silu_value).astype(jnp.bfloat16)

    def input_term(first_row, row_count):
        across = (((0,), (1,)), ((), ()))
        return lax.dot_general(
            w_gate, gate_grad, across, preferred_element_type=jnp.float32
        ) + lax.dot_general(w_up, up_grad, across, preferred_element_type=jnp.float32)

    term_sums = input_term(0, 0).astype(jnp.bfloat16)
    term_sums, gate_grad, up_grad, grad_slots = lax.optimization_barrier(
        (term_sums, gate_grad, up_grad, grad_slots)
    )
    input_sums = return_sums(term_sums, local_width, replicas, capacity)

    over_slots = (((0,), (0,)), ((), ()))
    grad_down = lax.dot_general(
        hidden, grad_slots, over_slots, preferred_element_type=jnp.float32
    ).astype(jnp.bfloat16)
    grad_gate = lax.dot_general(
        gate_grad, slot_rows, over_slots, preferred_element_type=jnp.float32
    ).astype(jnp.bfloat16)
    grad_up = lax.dot_general(
        up_grad, slot_rows, over_slots, preferred_element_type=jnp.float32
    ).astype(jnp.bfloat16)

    mixed_sum = lax.dot_general(
        mixing, expert_sums, rows_by_cols, precision=highest, preferred_element_type=jnp.float32
    )
    layer_out = (tokens.astype(jnp.float32) + mixed_sum).astype(jnp.bfloat16)
    returned = lax.dot_general(
        picker, input_sums, rows_by_cols, precision=highest, preferred_element_type=jnp.float32
    )
    grad_tokens = (grad_out.astype(jnp.float32) + returned).astype(jnp.bfloat16)
    return (layer_out, rewards, pair_loss, grad_tokens, grad_gate, grad_up, grad_down)


def solution(mesh):
    in_specs = (
        P("ep", "tp"),
        P("ep", None),
        P("ep"),
        P(("ep", "tp"), None),
        P(("ep", "tp"), None),
        P(("ep", "tp"), None),
        P("tp"),
        P("ep", "tp"),
        P(),
    )
    out_specs = (
        P("ep", "tp"),
        P(),
        P(),
        P("ep", "tp"),
        P(("ep", "tp"), None),
        P(("ep", "tp"), None),
        P(("ep", "tp"), None),
    )
    return jax.shard_map(
        per_device, mesh=mesh, in_specs=in_specs, out_specs=out_specs, check_vma=False
    )
```

time: 280 us -> 180 us (0.64)
  waiting for transfers between devices: 92.9 us -> 9.82 us
  blocking collectives: 73.1 us -> 0 us
  Pallas kernels: 0 us -> 38.5 us
  matrix products: 80 us -> 92.6 us
  other arithmetic: 3.33 us -> 6.94 us
    psum x1 -> x0, blocking collectives: 38.5 us -> none  [per_device(): rewards = lax.psum(placed, ('ep', 'tp'))]
    pallas_call x0 -> x2, Pallas kernels: none -> 38.5 us  [the longest x1 25.3 us: spread_slots(): pl.pallas_call(partial(spread_kernel, n_ep, n_tp), out_shape=(jax.ShapeDt...]
    all_gather x2 -> x1, waiting for transfers between devices: 36.1 us -> 0.01 us  [per_device(): lax.all_gather(ups_part, 'tp', axis=2, tiled=True).reshape(-1, width)]
    all_to_all x2 -> x0, blocking collectives: 34.5 us -> none  [gather_slots(): lax.all_to_all(buffer, 'ep', split_axis=0, concat_axis=0, tiled=True)]
    reduce_scatter x2, waiting for transfers between devices: 40.3 us -> 8.07 us  [return_sums(): lax.psum_scatter(sums, 'tp', scatter_dimension=0, tiled=True)]
    all_to_all x2, waiting for transfers between devices: 16.3 us -> 1.7 us  [return_sums(): lax.all_to_all(partial_sum.reshape(local_width, -1, capacity).astype(jnp....]
    dot_general x5 -> x2, matrix products: 11.6 us -> 18.6 us  [the longest x1 10.6 us: per_device(): lax.dot_general(ups_rows, w_down, rows_by_cols, preferred_element_type=jn...]
    dot_general x1, matrix products: 9.3 us -> 4.59 us  [input_term(): lax.dot_general(w_up, up_grad, across, preferred_element_type=jnp.float32)]
  transfers between devices with their start and end apart: 6 -> 5, of which waited for: 6 -> 2; matrix products, arithmetic and copies ran while one was open for 8% -> 53% of each run, Pallas kernels for 0% -> 7%
where the time goes in v1:
time: 180 us
  matrix products  92.6 us (51%)
  Pallas kernels  38.5 us (21%)
  between operations  15.9 us (9%)
  starting transfers between devices  11.7 us (6%)
  waiting for transfers between devices  9.82 us (5%)
  other arithmetic  6.94 us (4%)
  local copies, waits for them, and re-layouts  4.14 us (2%)
    pallas_call x1, Pallas kernels, spread_slots(): pl.pallas_call(partial(spread_kernel, n_ep, n_tp), out_shape=(jax.ShapeDt...  25.3 us
    dot_general x1, matrix products, per_device(): lax.dot_general(slot_rows, w_up, rows_by_cols, preferred_element_type=jnp...  14.9 us
    pallas_call x1, Pallas kernels, share_rows(): pl.pallas_call(partial(share_kernel, n_ep, n_tp), out_shape=jax.ShapeDtyp...  13.2 us
    all_to_all x2, starting transfers between devices, return_sums(): lax.all_to_all(partial_sum.reshape(local_width, -1, capacity).astype(jnp....  11.4 us
    dot_general x1, matrix products, per_device(): lax.dot_general(ups_rows, w_down, rows_by_cols, preferred_element_type=jn...  10.6 us
    dot_general x1, matrix products, per_device(): lax.dot_general(slot_rows, w_gate, rows_by_cols, preferred_element_type=j...  9.93 us
    dot_general x1, matrix products, down_term(): lax.dot_general(w_down, hidden, (((0,), (1,)), ((), ())), preferred_eleme...  9.44 us
    reduce_scatter x2, waiting for transfers between devices, return_sums(): lax.psum_scatter(sums, 'tp', scatter_dimension=0, tiled=True)  8.07 us
  transfers between devices with their start and end apart: 5, of which 2 were waited for; matrix products, arithmetic and copies ran while one was open for 53% of the time, Pallas kernels for 7%

profile of v1, /device:TPU:0, one launch (start us, length us, event | category | flops | bytes accessed | tf_op | source)
XLA Modules:
  0.0 179.5 jit_solution(2102578063148248935)
XLA Ops:
  7.2 0.8 subtract_bitcast_fusion
  8.0 0.8 slice_bitcast_fusion.1
  9.6 0.7 add_select_fusion
  10.3 0.7 maximum_select_fusion
  11.4 0.3 reduce_sum.166
  11.8 0.6 scatter.4.meta_ref
  12.5 1.0 convolution_convert_fusion.4
  13.5 1.0 convolution_convert_fusion.5
  14.6 25.3 %spread_slots.1 = (bf16[8,32,3072]{2,1,0:T(8,128)(2,1)}, bf16[8,32,768]{2,1,0:T(8,128)(2,1)}, f32[8,8,128]{2,1,0:T(8,128)}, f32[4,6,128]{2,1,0:T(8,128)}) custom-call(bf16[8,32,768]{2,1,0:T(8,128)(2,1)} %bitcast.60, bf16[8,32,768]{2,1,0:T(8,128)(2,1)} %bitcast.59, f32[8,8,128]{2,1,0:T(8,128)} %scatter.4.meta_ref, f32[6,128]{1,0:T(8,128)} %bitcast.65), custom_call_target="tpu_custom_call" | custom-call | tf_op jit(solution)/shard_map/spread_slots/pallas_call | solution.py:179
  40.2 9.9 %fusion.27 = f32[256,2048]{1,0:T(8,128)} fusion(bf16[256,3072]{1,0:T(8,128)(2,1)} %bitcast.53, bf16[2048,3072]{1,0:T(8,128)(2,1)} %param.14), kind=kOutput, calls=%fused_computation.79 | convolution fusion | flops 3221225472 | bytes 16252928 | tf_op jit(solution)/shard_map/dot_general | solution.py:291
  50.5 14.9 %multiply_convert_fusion.3 = (bf16[256,2048]{1,0:T(8,128)(2,1)S(1)}, f32[256,2048]{1,0:T(8,128)}) fusion(f32[256,2048]{1,0:T(8,128)} %fusion.27, bf16[256,3072]{1,0:T(8,128)(2,1)S(1)} %bitcast.54, bf16[2048,3072]{1,0:T(8,128)(2,1)} %param.15), kind=kOutput, calls=%fused_computation.15 | convolution fusion | flops 3224371200 | bytes 19398656 | tf_op jit(solution)/shard_map/dot_general | solution.py:292
  65.4 9.4 %fusion.1 = bf16[3072,256]{0,1:T(8,128)(2,1)} fusion(bf16[256,2048]{1,0:T(8,128)(2,1)S(1)} %get-tuple-element.56, bf16[2048,3072]{1,0:T(8,128)(2,1)} %param.16), kind=kOutput, calls=%fused_computation.6 | convolution fusion | flops 3222011904 | bytes 15204352 | tf_op jit(solution)/shard_map/dot_general | solution.py:297
  75.2 7.9 %convolution_reduce_fusion = f32[2048]{0:T(1024)S(1)} fusion(bf16[2048,3072]{1,0:T(8,128)(2,1)} %param.16, bf16[1,3072]{1,0:T(2,128)(2,1)S(1)} %stack.38, bf16[1,3072]{1,0:T(2,128)(2,1)S(1)} %stack.37, bf16[1,3072]{1,0:T(2,128)(2,1)S(1)} %stack.36), kind=kOutput, calls=%fused_computation.24 | convolution fusion | flops 37808128 | bytes 12609536 | tf_op jit(solution)/shard_map/dot_general | solution.py:313
  83.1 0.3 multiply_reduce_fusion
  83.8 0.6 pad_bitcast_fusion.mine_ref
  84.4 13.2 %share_rows.1 = f32[32,8,128]{2,1,0:T(8,128)} custom-call(f32[8,128]{1,0:T(8,128)} %pad_bitcast_fusion.mine_ref), custom_call_target="tpu_custom_call" | custom-call | tf_op jit(solution)/shard_map/share_rows/pallas_call | solution.py:236
  97.6 0.9 reduce_sum.172
  98.7 0.6 add_divide_fusion.1
  99.8 10.6 %multiply_convert_fusion.1 = (bf16[256,2048]{1,0:T(8,128)(2,1)S(1)}, bf16[256,2048]{1,0:T(8,128)(2,1)S(1)}) fusion(f32[256,2048]{1,0:T(8,128)} %fusion.27, f32[256,2048]{1,0:T(8,128)} %get-tuple-element.57, f32[2048]{0:T(1024)S(1)} %convolution_reduce_fusion, f32[256]{0:T(256)S(1)} %mul.197, bf16[256,3072]{1,0:T(8,128)(2,1)} %bitcast.61, ...), kind=kOutput, calls=%fused_computation.12 | convolution fusion | flops 3229614080 | bytes 20457472 | tf_op jit(solution)/shard_map/dot_general | solution.py:305
  110.5 0.7 multiply_convert_fusion
  111.3 7.4 %fusion.28 = f32[256,3072]{1,0:T(8,128)S(1)} fusion(bf16[256,2048]{1,0:T(8,128)(2,1)S(1)} %get-tuple-element.38, bf16[2048,3072]{1,0:T(8,128)(2,1)} %param.14), kind=kOutput, calls=%fused_computation.80 | convolution fusion | flops 3221225472 | bytes 16777216 | tf_op jit(solution)/shard_map/dot_general | solution.py:353
  118.7 0.8 slice-done.2
  119.5 4.6 %fusion.2 = bf16[3072,256]{0,1:T(8,128)(2,1)} fusion(f32[256,3072]{1,0:T(8,128)S(1)} %fusion.28, bf16[256,2048]{1,0:T(8,128)(2,1)S(1)} %get-tuple-element.39, bf16[2048,3072]{1,0:T(8,128)(2,1)S(1)} %bitcast.74), kind=kOutput, calls=%fused_computation.7 | convolution fusion | flops 3222798336 | bytes 18350080 | tf_op jit(solution)/shard_map/dot_general | solution.py:355
  124.1 7.9 %convolution_convert_fusion = bf16[2048,3072]{1,0:T(8,128)(2,1)} fusion(bf16[256,2048]{1,0:T(8,128)(2,1)} %copy-done.1, bf16[256,3072]{1,0:T(8,128)(2,1)S(1)} %multiply_convert_fusion), kind=kOutput, calls=%fused_computation | convolution fusion | flops 3227516928 | bytes 15204352 | tf_op jit(solution)/shard_map/dot_general | solution.py:364
  132.0 5.9 %all-to-all-start = ((bf16[768,8,32]{0,2,1:T(8,128)(2,1)}), bf16[768,8,32]{0,2,1:T(8,128)(2,1)S(1)}, u32[]{:S(2)}, u32[]{:S(2)}) async-start(bf16[768,8,32]{0,2,1:T(8,128)(2,1)} %bitcast.63), calls=%async_computation.1 | async-start | bytes 786432 | tf_op jit(solution)/shard_map/all_to_all | solution.py:254
  137.9 7.8 %convolution_convert_fusion.2 = bf16[2048,3072]{1,0:T(8,128)(2,1)} fusion(bf16[256,2048]{1,0:T(8,128)(2,1)} %copy-done.5, bf16[256,3072]{1,0:T(8,128)(2,1)S(1)} %bitcast.55), kind=kOutput, calls=%fused_computation.2 | convolution fusion | flops 3227516928 | bytes 15204352 | tf_op jit(solution)/shard_map/dot_general | solution.py:367
  145.7 8.1 %reduce-scatter.5.cloned.1.call-done = bf16[768,256]{0,1:T(8,128)(2,1)} async-done(((bf16[3072,256]{0,1:T(8,128)(2,1)}), bf16[768,256]{0,1:T(8,128)(2,1)}) %reduce-scatter.5.cloned.1.call-update) | async-done | bytes 393232 | tf_op jit(solution)/shard_map/reduce_scatter | solution.py:248
  153.8 5.5 %all-to-all-start.1 = ((bf16[768,8,32]{0,2,1:T(8,128)(2,1)}), bf16[768,8,32]{0,2,1:T(8,128)(2,1)S(1)}, u32[]{:S(2)}, u32[]{:S(2)}) async-start(bf16[768,8,32]{0,2,1:T(8,128)(2,1)} %bitcast.64), calls=%async_computation.3 | async-start | bytes 786432 | tf_op jit(solution)/shard_map/all_to_all | solution.py:254
  159.3 7.9 %convolution_convert_fusion.1 = bf16[2048,3072]{1,0:T(8,128)(2,1)} fusion(bf16[256,2048]{1,0:T(8,128)(2,1)} %copy-done.4, bf16[256,3072]{1,0:T(8,128)(2,1)S(1)} %bitcast.56), kind=kOutput, calls=%fused_computation.1 | convolution fusion | flops 3227516928 | bytes 15204352 | tf_op jit(solution)/shard_map/dot_general | solution.py:370
  168.1 1.0 fusion.5
  169.2 1.7 all-to-all-done.1
  170.9 1.0 fusion.6
  (79 shorter events, 3.6 us)
Async XLA Ops:
  7.2 5.3 %copy-start.8 = (bf16[128,768]{1,0:T(8,128)(2,1)S(1)}, bf16[128,768]{1,0:T(8,128)(2,1)}, u32[]{:S(2)}) copy-start(bf16[128,768]{1,0:T(8,128)(2,1)} %param.18) | copy-start | bytes 589828
  7.2 6.3 %copy-start.2 = (bf16[128,768]{1,0:T(8,128)(2,1)S(1)}, bf16[128,768]{1,0:T(8,128)(2,1)}, u32[]{:S(2)}) copy-start(bf16[128,768]{1,0:T(8,128)(2,1)} %param.11) | copy-start | bytes 589828
  7.2 67.7 %all-gather.2.cloned.1.call-start = ((), (), s32[]{:S(2)}) async-start(), calls=%async_computation.4 | async-start | bytes 1966080 | tf_op jit(solution)/shard_map/all_gather | solution.py:286
  9.6 30.4 %copy-start.14 = (s32[16]{0:T(128)S(1)}, s32[16]{0:T(128)}, u32[]{:S(2)}) copy-start(s32[16]{0:T(128)} %param.19) | copy-start | bytes 196
  11.1 29.1 %copy-start.6 = (f32[128,256]{1,0:T(8,128)}, f32[128,256]{1,0:T(8,128)S(1)}, u32[]{:S(2)}) copy-start(f32[128,256]{1,0:T(8,128)S(1)} %get-tuple-element.44) | copy-start | bytes 393220
  39.9 92.1 %reduce-scatter.3.cloned.1.call-start = ((), (), s32[]{:S(2)}) async-start(), calls=%async_computation.5 | async-start | bytes 1966080 | tf_op jit(solution)/shard_map/reduce_scatter | solution.py:248
  40.2 10.0 %copy-start.10 = (f32[768]{0:T(1024)S(1)}, f32[768]{0:T(1024)}, u32[]{:S(2)}) copy-start(f32[768]{0:T(1024)} %param.17) | copy-start | bytes 9220
  40.2 10.3 %copy-start.11 = (f32[4,6,128]{2,1,0:T(8,128)S(1)}, f32[4,6,128]{2,1,0:T(8,128)}, u32[]{:S(2)}) copy-start(f32[4,6,128]{2,1,0:T(8,128)} %get-tuple-element.32) | copy-start | bytes 36868
  40.2 10.3 %copy-start = (bf16[8,32,3072]{2,1,0:T(8,128)(2,1)S(1)}, bf16[8,32,3072]{2,1,0:T(8,128)(2,1)}, u32[]{:S(2)}) copy-start(bf16[8,32,3072]{2,1,0:T(8,128)(2,1)} %get-tuple-element.30) | copy-start | bytes 4718596
  65.4 17.7 %copy-start.1 = (bf16[256,2048]{1,0:T(8,128)(2,1)}, bf16[256,2048]{1,0:T(8,128)(2,1)S(1)}, u32[]{:S(2)}) copy-start(bf16[256,2048]{1,0:T(8,128)(2,1)S(1)} %get-tuple-element.56) | copy-start | bytes 3145732
  74.9 78.9 %reduce-scatter.5.cloned.1.call-start = ((), (), s32[]{:S(2)}) async-start(), calls=%async_computation.6 | async-start | bytes 1966080 | tf_op jit(solution)/shard_map/reduce_scatter | solution.py:248
  75.2 8.3 %copy-start.12 = (f32[8,8,128]{2,1,0:T(8,128)S(1)}, f32[8,8,128]{2,1,0:T(8,128)}, u32[]{:S(2)}) copy-start(f32[8,8,128]{2,1,0:T(8,128)} %get-tuple-element.34) | copy-start | bytes 98308
  98.6 11.9 %copy-start.13 = (f32[16]{0:T(128)}, f32[16]{0:T(128)S(1)}, u32[]{:S(2)}) copy-start(f32[16]{0:T(128)S(1)} %slice_multiply_fusion) | copy-start | bytes 196
  99.8 10.6 %copy-start.3 = (bf16[8,32,3072]{2,1,0:T(8,128)(2,1)S(1)}, bf16[8,32,3072]{2,1,0:T(8,128)(2,1)}, u32[]{:S(2)}) copy-start(bf16[8,32,3072]{2,1,0:T(8,128)(2,1)} %all-gather.2.cloned.1.call-done) | copy-start | bytes 4718596
  110.5 8.2 %copy-start.5 = (bf16[256,2048]{1,0:T(8,128)(2,1)}, bf16[256,2048]{1,0:T(8,128)(2,1)S(1)}, u32[]{:S(2)}) copy-start(bf16[256,2048]{1,0:T(8,128)(2,1)S(1)} %get-tuple-element.38) | copy-start | bytes 3145732
  110.5 8.2 %copy-start.4 = (bf16[256,2048]{1,0:T(8,128)(2,1)}, bf16[256,2048]{1,0:T(8,128)(2,1)S(1)}, u32[]{:S(2)}) copy-start(bf16[256,2048]{1,0:T(8,128)(2,1)S(1)} %get-tuple-element.39) | copy-start | bytes 3145732
  110.5 8.2 %slice-start = ((s8[12582912]{0:T(1024)(128)(4,1)}), s8[4194304]{0:T(1024)(128)(4,1)S(1)}, s32[]{:S(2)}) async-start(s8[12582912]{0:T(1024)(128)(4,1)} %bitcast.73), calls=%async_computation.7 | async-start | bytes 8388608
  111.2 7.5 %slice-start.1 = ((s8[12582912]{0:T(1024)(128)(4,1)}), s8[4194304]{0:T(1024)(128)(4,1)S(1)}, s32[]{:S(2)}) async-start(s8[12582912]{0:T(1024)(128)(4,1)} %bitcast.73), calls=%async_computation.8 | async-start | bytes 8388608
  111.3 8.2 %slice-start.2 = ((s8[12582912]{0:T(1024)(128)(4,1)}), s8[4194304]{0:T(1024)(128)(4,1)S(1)}, s32[]{:S(2)}) async-start(s8[12582912]{0:T(1024)(128)(4,1)} %bitcast.73), calls=%async_computation.9 | async-start | bytes 8388608
  132.0 21.8 %all-to-all-start = ((bf16[768,8,32]{0,2,1:T(8,128)(2,1)}), bf16[768,8,32]{0,2,1:T(8,128)(2,1)S(1)}, u32[]{:S(2)}, u32[]{:S(2)}) async-start(bf16[768,8,32]{0,2,1:T(8,128)(2,1)} %bitcast.63), calls=%async_computation.1 | async-start | bytes 786432 | tf_op jit(solution)/shard_map/all_to_all | solution.py:254
  153.8 17.0 %all-to-all-start.1 = ((bf16[768,8,32]{0,2,1:T(8,128)(2,1)}), bf16[768,8,32]{0,2,1:T(8,128)(2,1)S(1)}, u32[]{:S(2)}, u32[]{:S(2)}) async-start(bf16[768,8,32]{0,2,1:T(8,128)(2,1)} %bitcast.64), calls=%async_computation.3 | async-start | bytes 786432 | tf_op jit(solution)/shard_map/all_to_all | solution.py:254
  159.3 8.8 %copy-start.7 = (f32[128,256]{1,0:T(8,128)S(1)}, f32[128,256]{1,0:T(8,128)}, u32[]{:S(2)}) copy-start(f32[128,256]{1,0:T(8,128)} %copy-done.6) | copy-start | bytes 393220
  159.3 11.5 %copy-start.9 = (bf16[128,768]{1,0:T(8,128)(2,1)S(1)}, bf16[128,768]{1,0:T(8,128)(2,1)}, u32[]{:S(2)}) copy-start(bf16[128,768]{1,0:T(8,128)(2,1)} %param.18) | copy-start | bytes 589828
Sparse Core Ops, SparseCore 0:
  40.0 24.5 all-gather.1
  75.0 32.6 reduce-scatter.2
  124.2 29.5 reduce-scatter.4
